TPU v7x, 32 devices: a whole 2x2x4 slice. The times are simulated.
32 devices in a mesh: mesh: 8 (over z, y), pts: 4 (over x, core).
Axes of the slice: x: 2, y: 2, z: 4, core: 2. Of those that a mesh axis runs over, the one named last changes fastest.
Arguments:
- inputs: float32 [32768, 8], P(('mesh', 'pts')), may hold values from -6 to 6
- target: float32 [32768, 4], P(('mesh', 'pts')), may hold values from -6 to 6
- lengths: int32 [8, 4], P('mesh'), may hold values from 1 to 2048, 4096 in all within a row
- step_count: int32 [1], replicated, may hold values from 2 to 20
- muon_weight: float32 [2, 5, 256, 256], P(None, None, ('mesh', 'pts')), may hold values from -0.375 to 0.375
- muon_moment: float32 [2, 5, 256, 256], P(None, None, ('mesh', 'pts')), may hold values from -0.0017089844 to 0.0017089844
- adam_weight: float32 [18848], P(('mesh', 'pts'))
- adam_first: float32 [18848], P(('mesh', 'pts')), may hold values from -0.0004272461 to 0.0004272461
- adam_second: float32 [18848], P(('mesh', 'pts')), may hold values from 2e-11 to 4e-09
Outputs:
- new_muon_weight: float32 [2, 5, 256, 256], P(None, None, ('mesh', 'pts'))
- new_muon_moment: float32 [2, 5, 256, 256], P(None, None, ('mesh', 'pts'))
- new_adam_weight: float32 [18848], P(('mesh', 'pts'))
- new_adam_first: float32 [18848], P(('mesh', 'pts'))
- new_adam_second: float32 [18848], P(('mesh', 'pts'))
- step_loss: float32 [], replicated
- clip_norm: float32 [], replicated
Inputs may be any that keep to these rules, and one draw needn't show every extreme that they name: Each group's 4 lengths sum to 4096, and the largest of each group is exactly half of that.
All inputs are finite; a program needn't handle non-finite values.
Results may differ from a plain program's by a relative error of at most 0.0003.
Values sent between devices are 32-bit elements; how exact they have to be, the bound alone decides.
A program may use at most 192 MiB of HBM per device.

v0:
```python
from functools import partial
import math

import jax
import jax.numpy as jnp
from jax import lax
from jax.sharding import PartitionSpec as P

C = 256
H = 8
DH = 32
S = 64
IN = 8
OUT = 4
L = 2


HIGH = lax.Precision.HIGHEST
ns_a = 3.4445
ns_b = -4.775
ns_c = 2.0315
peak_rate = 0.3
warm_steps = 12.0
total_steps = 40.0


def layout():
    pieces = [
        ("emb_w", (IN, C)),
        ("emb_b", (C,)),
        ("head_w", (C, OUT)),
        ("head_b", (OUT,)),
        ("fin", (2, C)),
        ("qkv", (L, 3, DH, DH)),
        ("slice_w", (L, DH, S)),
        ("slice_b", (L, S)),
        ("temp", (L, H)),
        ("vec", (L, 9, C)),
    ]
    places = {}
    offset = 0
    for label_text, extent in pieces:
        places[label_text] = (offset, extent)
        offset = offset + math.prod(extent)
    return places


def unpack(packed):
    return {
        label_text: packed[offset : offset + math.prod(extent)].reshape(extent)
        for label_text, (offset, extent) in layout().items()
    }


def matmul(left, right):
    return jnp.dot(left, right, precision=HIGH)


def norm_rows(values, gain, shift):
    centre = values - jnp.mean(values, axis=-1, keepdims=True)
    spread = jnp.mean(centre * centre, axis=-1, keepdims=True)
    return centre * lax.rsqrt(spread + 1e-05) * gain + shift


def mesh_mask(lengths_row, first, points):
    ends = jnp.cumsum(lengths_row)
    starts = ends - lengths_row
    position = first + jnp.arange(points, dtype=jnp.int32)
    inside = (position[:, None] >= starts[None, :]) & (position[:, None] < ends[None, :])
    return inside.astype(jnp.float32)


def embed_piece(inputs, packed):
    params = unpack(packed)
    return matmul(inputs, params["emb_w"]) + params["emb_b"]


def slice_piece(hidden, matrices, packed, layer_index, onehot):
    params = unpack(packed)
    vectors = params["vec"][layer_index]
    points = hidden.shape[0]
    normed = norm_rows(hidden, vectors[0], vectors[1])
    features = (matmul(normed, matrices[0]) + vectors[2]).reshape(points, H, DH)
    routed = (matmul(normed, matrices[1]) + vectors[3]).reshape(points, H, DH)
    logits = jnp.einsum("phd,ds->phs", routed, params["slice_w"][layer_index], precision=HIGH)
    logits = (logits + params["slice_b"][layer_index]) / params["temp"][layer_index][:, None]
    weights = jax.nn.softmax(logits, axis=-1)
    numerator = jnp.einsum("pm,phs,phd->mhsd", onehot, weights, features, precision=HIGH)
    denominator = jnp.einsum("pm,phs->mhs", onehot, weights, precision=HIGH)
    return (weights, numerator, denominator)


def mix_piece(numerator, denominator, packed, layer_index):
    triple = unpack(packed)["qkv"][layer_index]
    tokens = numerator / (denominator[..., None] + 1e-05)
    queries = jnp.einsum("mhsd,de->mhse", tokens, triple[0], precision=HIGH)
    keys_all = jnp.einsum("mhsd,de->mhse", tokens, triple[1], precision=HIGH)
    values = jnp.einsum("mhsd,de->mhse", tokens, triple[2], precision=HIGH)
    scores = jnp.einsum("mhsd,mhtd->mhst", queries, keys_all, precision=HIGH) * DH ** (-0.5)
    return jnp.einsum("mhst,mhtd->mhsd", jax.nn.softmax(scores, axis=-1), values, precision=HIGH)


def out_piece(hidden, weights, mixed, matrices, packed, layer_index, onehot):
    vectors = unpack(packed)["vec"][layer_index]
    points = hidden.shape[0]
    spread_wts = onehot[:, :, None, None] * weights[:, None, :, :]
    pointwise = jnp.einsum("pmhs,mhsd->phd", spread_wts, mixed, precision=HIGH).reshape(points, C)
    hidden = hidden + matmul(pointwise, matrices[2]) + vectors[4]
    normed = norm_rows(hidden, vectors[5], vectors[6])
    inner = jax.nn.gelu(matmul(normed, matrices[3]) + vectors[7], approximate=False)
    return hidden + matmul(inner, matrices[4]) + vectors[8]


def head_piece(hidden, packed, target, onehot):
    params = unpack(packed)
    normed = norm_rows(hidden, params["fin"][0], params["fin"][1])
    predicted = matmul(normed, params["head_w"]) + params["head_b"]
    misfit = predicted - target
    errors = matmul(onehot.T, jnp.sum(misfit * misfit, axis=-1))
    scales = matmul(onehot.T, jnp.sum(target * target, axis=-1))
    return (errors, scales)


def loss_piece(errors, scales, meshes, floor_value):
    return jnp.sum(jnp.sqrt((errors + 1e-06) / jnp.maximum(scales, floor_value))) / meshes


def one_cycle(count):
    start_rate = peak_rate / 25.0
    end_rate = start_rate / 10000.0
    rising = start_rate + (peak_rate - start_rate) * 0.5 * (
        1.0 - jnp.cos(math.pi * count / warm_steps)
    )
    falling = end_rate + (peak_rate - end_rate) * 0.5 * (
        1.0 + jnp.cos(math.pi * (count - warm_steps) / (total_steps - warm_steps))
    )
    return jnp.where(count <= warm_steps, rising, falling)


def newton_schulz(current, gram_of):
    for sweep in range(5):
        gram = gram_of(current)
        product = jnp.einsum("...rc,...cd->...rd", current, gram, precision=HIGH)
        current = (
            ns_a * current
            + ns_b * product
            + ns_c * jnp.einsum("...rc,...cd->...rd", product, gram, precision=HIGH)
        )
    return current


def apply_update(
    grad_muon,
    grad_adam,
    square_sum,
    step_count,
    muon_weight,
    muon_moment,
    adam_weight,
    adam_first,
    adam_second,
    frob_of,
    orthogonal_of,
):
    norm_value = jnp.sqrt(square_sum)
    factor = 0.1 / jnp.maximum(norm_value, 0.1)
    moment = 0.95 * muon_moment + factor * grad_muon
    normalized = moment / (jnp.sqrt(frob_of(moment)) + 1e-07)[..., None, None]
    current = orthogonal_of(normalized)
    count = step_count[0].astype(jnp.float32)
    rate = one_cycle(count)
    new_muon = muon_weight * (1.0 - rate * 0.01) - rate * (0.2 * C**0.5) * current
    clipped = factor * grad_adam
    first = 0.9 * adam_first + 0.1 * clipped
    second = 0.999 * adam_second + 0.001 * clipped * clipped
    first_hat = first / (1.0 - 0.9**count)
    second_hat = second / (1.0 - 0.999**count)
    new_adam = adam_weight * (1.0 - rate * 0.01) - rate * first_hat / (jnp.sqrt(second_hat) + 1e-08)
    return (new_muon, moment, new_adam, first, second, norm_value)


def local(
    inputs,
    target,
    lengths,
    step_count,
    muon_weight,
    muon_moment,
    adam_weight,
    adam_first,
    adam_second,
):
    muon_all, adam_all = (
        lax.all_gather(muon_weight, ("mesh", "pts"), axis=2, tiled=True),
        lax.all_gather(adam_weight, ("mesh", "pts"), axis=0, tiled=True),
    )
    points = inputs.shape[0]
    pts_count = lax.axis_size("pts")
    floor_value = float(points * pts_count)
    onehot = mesh_mask(lengths[0], lax.axis_index("pts") * points, points)
    meshes = lax.axis_size("mesh") * lengths.shape[1]
    hidden, embed_back = jax.vjp(lambda packed: embed_piece(inputs, packed), adam_all)
    saved = []
    for layer_index in range(L):
        matrices = muon_all[layer_index]
        (weights, numerator, denominator), slice_back = jax.vjp(
            partial(slice_piece, layer_index=layer_index, onehot=onehot), hidden, matrices, adam_all
        )
        numerator, denominator = lax.psum((numerator, denominator), "pts")
        mixed, mix_back = jax.vjp(
            partial(mix_piece, layer_index=layer_index), numerator, denominator, adam_all
        )
        following, out_back = jax.vjp(
            partial(out_piece, layer_index=layer_index, onehot=onehot),
            hidden,
            weights,
            mixed,
            matrices,
            adam_all,
        )
        saved.append((slice_back, mix_back, out_back))
        hidden = following
    (errors, scales), head_back = jax.vjp(
        lambda state, packed: head_piece(state, packed, target, onehot), hidden, adam_all
    )
    errors, scales = lax.psum((errors, scales), "pts")
    group_loss, loss_back = jax.vjp(
        lambda first, second: loss_piece(first, second, meshes, floor_value), errors, scales
    )
    grad_errors, grad_scales = loss_back(jnp.ones_like(group_loss))
    grad_hidden, grad_adam = head_back((grad_errors, grad_scales))
    grad_layers = [None] * L
    for layer_index in reversed(range(L)):
        slice_back, mix_back, out_back = saved[layer_index]
        grad_hidden_out, grad_weights, grad_mixed, grad_mats_out, grad_adam_out = out_back(
            grad_hidden
        )
        grad_mixed = lax.psum(grad_mixed, "pts")
        grad_num, grad_den, grad_adam_mix = mix_back(grad_mixed)
        grad_hidden_in, grad_mats_in, grad_adam_in = slice_back((grad_weights, grad_num, grad_den))
        grad_hidden = grad_hidden_out + grad_hidden_in
        grad_adam = grad_adam + grad_adam_out + grad_adam_in + grad_adam_mix / pts_count
        grad_layers[layer_index] = grad_mats_out + grad_mats_in
    (grad_embed,) = embed_back(grad_hidden)
    grad_adam = grad_adam + grad_embed
    grad_muon = jnp.stack(grad_layers)
    grad_muon, grad_adam = (
        lax.psum_scatter(grad_muon, ("mesh", "pts"), scatter_dimension=2, tiled=True),
        lax.psum_scatter(grad_adam, ("mesh", "pts"), scatter_dimension=0, tiled=True),
    )
    square_sum, loss_total = lax.psum(
        (jnp.sum(grad_muon * grad_muon) + jnp.sum(grad_adam * grad_adam), group_loss / pts_count),
        ("mesh", "pts"),
    )

    def frob_of(moment):
        return lax.psum(jnp.sum(moment * moment, axis=(2, 3)), ("mesh", "pts"))

    def orthogonal_of(normalized):
        groups = lax.axis_size("mesh")
        count_all = normalized.shape[0] * normalized.shape[1]
        per_group = (count_all + groups - 1) // groups
        stacked = normalized.reshape((count_all,) + normalized.shape[2:])
        filler = jnp.zeros((per_group * groups - count_all,) + normalized.shape[2:], jnp.float32)
        spread = lax.all_to_all(
            jnp.concatenate([stacked, filler], axis=0),
            "mesh",
            split_axis=0,
            concat_axis=1,
            tiled=True,
        )

        def gram_of(current):
            return lax.psum(jnp.einsum("krc,krd->kcd", current, current, precision=HIGH), "pts")

        finished = newton_schulz(spread, gram_of)
        returned = lax.all_to_all(finished, "mesh", split_axis=1, concat_axis=0, tiled=True)
        return returned[:count_all].reshape(normalized.shape)

    results = apply_update(
        grad_muon,
        grad_adam,
        square_sum,
        step_count,
        muon_weight,
        muon_moment,
        adam_weight,
        adam_first,
        adam_second,
        frob_of,
        orthogonal_of,
    )
    return (results[0], results[1], results[2], results[3], results[4], loss_total, results[5])


def solution(mesh):
    in_specs = (
        P(("mesh", "pts"), None),
        P(("mesh", "pts"), None),
        P("mesh", None),
        P(),
        P(None, None, ("mesh", "pts"), None),
        P(None, None, ("mesh", "pts"), None),
        P(("mesh", "pts")),
        P(("mesh", "pts")),
        P(("mesh", "pts")),
    )
    out_specs = (
        P(None, None, ("mesh", "pts"), None),
        P(None, None, ("mesh", "pts"), None),
        P(("mesh", "pts")),
        P(("mesh", "pts")),
        P(("mesh", "pts")),
        P(),
        P(),
    )
    return jax.shard_map(local, mesh=mesh, in_specs=in_specs, out_specs=out_specs, check_vma=False)
```

profile of v0, /device:TPU:0, one launch (start us, length us, event | category | flops | bytes accessed | tf_op | source)
XLA Modules:
  0.0 1214.7 jit_solution(13003831298324453706)
XLA Ops:
  12.7 125.0 %all-reduce.100.cloned.1.call-done = f32[18848]{0:T(1024)} async-done(((f32[18848]{0:T(1024)}), f32[18848]{0:T(1024)}) %all-reduce.100.cloned.1.call-update) | async-done | bytes 75408
  154.3 45.1 %all-gather.2.cloned.1.call-done = f32[2,5,256,256]{3,2,1,0:T(8,128)} async-done(((f32[2,5,8,256]{3,2,1,0:T(8,128)}), f32[2,5,256,256]{3,2,1,0:T(8,128)}) %all-gather.2.cloned.1.call-update) | async-done | bytes 2621456 | tf_op jit(solution)/shard_map/all_gather | solution.py:194
  206.6 11.2 psum.113
  222.3 4.7 fusion.42
  230.0 29.2 %all-reduce.82.cloned.1.call-done = f32[4,8,64,32]{2,3,0,1:T(8,128)} async-done(((f32[4,8,64,32]{2,3,0,1:T(8,128)}), f32[4,8,64,32]{2,3,0,1:T(8,128)}) %all-reduce.82.cloned.1.call-update) | async-done | bytes 262160 | tf_op jit(solution)/shard_map/psum | solution.py:209
  267.7 5.2 fusion.2
  275.6 5.0 fusion.58
  291.1 10.1 psum.115
  305.7 4.7 fusion.47
  311.4 32.7 %all-reduce.84.cloned.1.call-done = f32[4,8,64,32]{2,3,0,1:T(8,128)} async-done(((f32[4,8,64,32]{2,3,0,1:T(8,128)}), f32[4,8,64,32]{2,3,0,1:T(8,128)}) %all-reduce.84.cloned.1.call-update) | async-done | bytes 262160 | tf_op jit(solution)/shard_map/psum | solution.py:209
  353.1 5.2 fusion
  360.8 5.2 fusion.59
  371.2 5.7 all-reduce.69
  412.1 12.3 %fusion.40 = f32[4,8,64,32]{2,3,0,1:T(8,128)} fusion(f32[8,32,1024,1]{2,1,3,0:T(8,128)S(1)} %convolution_bitcast_fusion.1, f32[1024,8,64]{0,2,1:T(8,128)S(1)} %copy-done.16, f32[1024,4]{0,1:T(4,128)S(1)} %copy-done.107), kind=kOutput, calls=%fused_computation.83 | convolution fusion | flops 807403520 | bytes 3424256 | tf_op jit(solution)/shard_map/transpose(jvp(pmhs,mhsd->phd))/dot_general | solution.py:107
  424.3 10.0 multiply_reduce_fusion.1
  444.1 23.9 %all-reduce.86.cloned.1.call-done = f32[4,8,64,32]{2,3,0,1:T(8,128)} async-done(((f32[4,8,64,32]{2,3,0,1:T(8,128)}), f32[4,8,64,32]{2,3,0,1:T(8,128)}) %all-reduce.86.cloned.1.call-update) | async-done | bytes 262160 | tf_op jit(solution)/shard_map/psum | solution.py:238
  480.1 4.8 fusion.13
  528.7 12.4 %fusion.41 = f32[4,8,64,32]{2,3,0,1:T(8,128)} fusion(f32[8,32,1024,1]{2,1,3,0:T(8,128)S(1)} %convolution_bitcast_fusion, f32[1024,8,64]{0,2,1:T(8,128)S(1)} %copy-done.9, f32[1024,4]{0,1:T(4,128)S(1)} %copy-done.109), kind=kOutput, calls=%fused_computation.84 | convolution fusion | flops 807403520 | bytes 3424256 | tf_op jit(solution)/shard_map/transpose(jvp(pmhs,mhsd->phd))/dot_general | solution.py:107
  541.1 9.7 multiply_reduce_fusion
  572.4 30.5 %all-reduce.88.cloned.1.call-done = f32[4,8,64,32]{2,3,0,1:T(8,128)} async-done(((f32[4,8,64,32]{2,3,0,1:T(8,128)}), f32[4,8,64,32]{2,3,0,1:T(8,128)}) %all-reduce.88.cloned.1.call-update) | async-done | bytes 262160 | tf_op jit(solution)/shard_map/psum | solution.py:238
  647.0 117.6 %all-reduce.102.cloned.1.call-done = f32[18848]{0:T(1024)} async-done(((f32[18848]{0:T(1024)}), f32[18848]{0:T(1024)}) %all-reduce.102.cloned.1.call-update) | async-done | bytes 75408
  766.0 142.6 %reduce-scatter.2.cloned.1.call-done = f32[2,5,8,256]{3,2,1,0:T(8,128)} async-done(((f32[2,5,256,256]{3,2,1,0:T(8,128)}), f32[2,5,8,256]{3,2,1,0:T(8,128)}) %reduce-scatter.2.cloned.1.call-update) | async-done | bytes 81936 | tf_op jit(solution)/shard_map/reduce_scatter | solution.py:248
  912.0 36.8 %psum.120 = f32[]{:T(128)} all-reduce(f32[]{:T(128)S(6)} %add.556), channel_id=1, replica_groups=mesh['mesh'=8,'pts'=4] {'mesh','pts'}, use_global_device_ids=true, to_apply=%region_77.78 | all-reduce | flops 1 | bytes 8 | tf_op jit(solution)/shard_map/psum | solution.py:251
  950.6 41.2 %all-reduce.68 = (f32[2,5]{1,0:T(2,128)S(1)}, f32[]{:T(128)}) all-reduce(f32[2,5]{1,0:T(2,128)S(1)} %get-tuple-element.29, f32[]{:T(128)S(6)} %div.387), channel_id=1, replica_groups=mesh['mesh'=8,'pts'=4] {'mesh','pts'}, use_global_device_ids=true, to_apply=%region_79.80 | all-reduce | flops 11 | bytes 88 | tf_op jit(solution)/shard_map/psum | solution.py:257
  991.9 11.9 all_to_all.33
  1005.3 31.6 %all-reduce.90.cloned.1.call-done = f32[2,256,256]{2,1,0:T(8,128)} async-done(((f32[2,256,256]{2,1,0:T(8,128)}), f32[2,256,256]{2,1,0:T(8,128)}) %all-reduce.90.cloned.1.call-update) | async-done | bytes 524304 | tf_op jit(solution)/shard_map/psum | solution.py:274
  1041.4 33.6 %all-reduce.92.cloned.1.call-done = f32[2,256,256]{2,1,0:T(8,128)} async-done(((f32[2,256,256]{2,1,0:T(8,128)}), f32[2,256,256]{2,1,0:T(8,128)}) %all-reduce.92.cloned.1.call-update) | async-done | bytes 524304 | tf_op jit(solution)/shard_map/psum | solution.py:274
  1079.5 33.6 %all-reduce.94.cloned.1.call-done = f32[2,256,256]{2,1,0:T(8,128)} async-done(((f32[2,256,256]{2,1,0:T(8,128)}), f32[2,256,256]{2,1,0:T(8,128)}) %all-reduce.94.cloned.1.call-update) | async-done | bytes 524304 | tf_op jit(solution)/shard_map/psum | solution.py:274
  1117.9 33.4 %all-reduce.96.cloned.1.call-done = f32[2,256,256]{2,1,0:T(8,128)} async-done(((f32[2,256,256]{2,1,0:T(8,128)}), f32[2,256,256]{2,1,0:T(8,128)}) %all-reduce.96.cloned.1.call-update) | async-done | bytes 524304 | tf_op jit(solution)/shard_map/psum | solution.py:274
  1155.8 33.7 %all-reduce.98.cloned.1.call-done = f32[2,256,256]{2,1,0:T(8,128)} async-done(((f32[2,256,256]{2,1,0:T(8,128)}), f32[2,256,256]{2,1,0:T(8,128)}) %all-reduce.98.cloned.1.call-update) | async-done | bytes 524304 | tf_op jit(solution)/shard_map/psum | solution.py:274
  1193.2 5.5 all-to-all-start.1
  1201.1 5.0 all-to-all-done.1
  (716 shorter events, 273.3 us)
Async XLA Ops:
  7.2 141.5 %copy-start = (f32[1024,8]{0,1:T(8,128)S(1)}, f32[1024,8]{0,1:T(8,128)}, u32[]{:S(2)}) copy-start(f32[1024,8]{0,1:T(8,128)} %param.9) | copy-start | bytes 98308
  7.2 130.6 %all-reduce.100.cloned.1.call-start = ((), (), s32[]{:S(2)}) async-start(), calls=%async_computation.14 | async-start | bytes 155648
  8.8 190.7 %all-gather.2.cloned.1.call-start = ((), (), s32[]{:S(2)}) async-start(), calls=%async_computation.3 | async-start | bytes 2703360 | tf_op jit(solution)/shard_map/all_gather | solution.py:194
  9.6 249.7 %all-reduce.82.cloned.1.call-start = ((), (), s32[]{:S(2)}) async-start(), calls=%async_computation.4 | async-start | bytes 1048576 | tf_op jit(solution)/shard_map/psum | solution.py:209
  10.4 279.2 %copy-start.153 = (s32[4,1]{0,1:T(1,128)}, s32[4,1]{0,1:T(1,128)S(1)}, u32[]{:S(2)}) copy-start(s32[4,1]{0,1:T(1,128)S(1)} %reduce-window.4) | copy-start | bytes 52
  11.8 277.8 %copy-start.156 = (s32[4]{0:T(128)}, s32[4]{0:T(128)S(1)}, u32[]{:S(2)}) copy-start(s32[4]{0:T(128)S(1)} %fusion.197) | copy-start | bytes 52
  11.9 189.8 %copy-start.192 = (pred[4,1024]{1,0:T(4,128)(4,1)}, pred[4,1024]{1,0:T(4,128)(4,1)S(1)}, u32[]{:S(2)}) copy-start(pred[4,1024]{1,0:T(4,128)(4,1)S(1)} %compare_and_fusion) | copy-start | bytes 12292
  12.7 339.9 %copy-start.106 = (f32[1024,4]{0,1:T(4,128)}, f32[1024,4]{0,1:T(4,128)S(1)}, u32[]{:S(2)}) copy-start(f32[1024,4]{0,1:T(4,128)S(1)} %fusion.222) | copy-start | bytes 49156
  146.4 139.2 %copy-start.129 = (f32[32,64,1]{1,0,2:T(8,128)}, f32[32,64,1]{1,0,2:T(8,128)S(1)}, u32[]{:S(2)}) copy-start(f32[32,64,1]{1,0,2:T(8,128)S(1)} %reshape.745) | copy-start | bytes 24580
  146.5 55.3 %copy-start.124 = (f32[32,64,1]{1,0,2:T(8,128)}, f32[32,64,1]{1,0,2:T(8,128)S(1)}, u32[]{:S(2)}) copy-start(f32[32,64,1]{1,0,2:T(8,128)S(1)} %reshape.738) | copy-start | bytes 24580
  148.6 70.4 %copy-start.137 = (f32[256]{0:T(256)}, f32[256]{0:T(256)S(1)}, u32[]{:S(2)}) copy-start(f32[256]{0:T(256)S(1)} %get-tuple-element.83) | copy-start | bytes 3076
  149.8 54.1 %copy-start.139 = (f32[1024]{0:T(1024)}, f32[1024]{0:T(1024)S(1)}, u32[]{:S(2)}) copy-start(f32[1024]{0:T(1024)S(1)} %multiply_reduce_fusion.22) | copy-start | bytes 12292
  151.2 53.2 %copy-start.175 = (f32[64]{0:T(128)}, f32[64]{0:T(128)S(1)}, u32[]{:S(2)}) copy-start(f32[64]{0:T(128)S(1)} %get-tuple-element.79) | copy-start | bytes 772
  152.6 51.9 %copy-start.177 = (f32[8]{0:T(128)}, f32[8]{0:T(128)S(1)}, u32[]{:S(2)}) copy-start(f32[8]{0:T(128)S(1)} %get-tuple-element.51) | copy-start | bytes 100
  154.3 64.8 %copy-start.147 = (f32[256]{0:T(256)}, f32[256]{0:T(256)S(1)}, u32[]{:S(2)}) copy-start(f32[256]{0:T(256)S(1)} %get-tuple-element.70) | copy-start | bytes 3076
  154.3 121.2 %copy-start.151 = (f32[256]{0:T(256)}, f32[256]{0:T(256)S(1)}, u32[]{:S(2)}) copy-start(f32[256]{0:T(256)S(1)} %get-tuple-element.66) | copy-start | bytes 3076
  154.3 148.1 %copy-start.135 = (f32[256]{0:T(256)}, f32[256]{0:T(256)S(1)}, u32[]{:S(2)}) copy-start(f32[256]{0:T(256)S(1)} %get-tuple-element.62) | copy-start | bytes 3076
  154.3 148.1 %copy-start.149 = (f32[256]{0:T(256)}, f32[256]{0:T(256)S(1)}, u32[]{:S(2)}) copy-start(f32[256]{0:T(256)S(1)} %get-tuple-element.61) | copy-start | bytes 3076
  205.3 62.4 %copy-start.8 = (f32[1024,8,64]{0,2,1:T(8,128)}, f32[1024,8,64]{0,2,1:T(8,128)S(1)}, u32[]{:S(2)}) copy-start(f32[1024,8,64]{0,2,1:T(8,128)S(1)} %fusion.36) | copy-start | bytes 6291460
  227.0 117.2 %all-reduce.84.cloned.1.call-start = ((), (), s32[]{:S(2)}) async-start(), calls=%async_computation.5 | async-start | bytes 1048576 | tf_op jit(solution)/shard_map/psum | solution.py:209
  310.4 157.6 %all-reduce.86.cloned.1.call-start = ((), (), s32[]{:S(2)}) async-start(), calls=%async_computation.6 | async-start | bytes 1048576 | tf_op jit(solution)/shard_map/psum | solution.py:238
  434.3 168.6 %all-reduce.88.cloned.1.call-start = ((), (), s32[]{:S(2)}) async-start(), calls=%async_computation.7 | async-start | bytes 1048576 | tf_op jit(solution)/shard_map/psum | solution.py:238
  569.2 195.4 %all-reduce.102.cloned.1.call-start = ((), (), s32[]{:S(2)}) async-start(), calls=%async_computation.15 | async-start | bytes 155648
  643.5 265.1 %reduce-scatter.2.cloned.1.call-start = ((), (), s32[]{:S(2)}) async-start(), calls=%async_computation.8 | async-start | bytes 2703360 | tf_op jit(solution)/shard_map/reduce_scatter | solution.py:248
  645.7 303.9 %copy-start.114 = (f32[2,5,8,256]{3,2,1,0:T(8,128)S(1)}, f32[2,5,8,256]{3,2,1,0:T(8,128)}, u32[]{:S(2)}) copy-start(f32[2,5,8,256]{3,2,1,0:T(8,128)} %param.14) | copy-start | bytes 245764
  645.7 391.2 %all-reduce.90.cloned.1.call-start = ((), (), s32[]{:S(2)}) async-start(), calls=%async_computation.9 | async-start | bytes 1048576 | tf_op jit(solution)/shard_map/psum | solution.py:274
  950.6 90.8 %copy-start.93 = (f32[2,5,8,256]{3,2,1,0:T(8,128)}, f32[2,5,8,256]{3,2,1,0:T(8,128)S(1)}, u32[]{:S(2)}) copy-start(f32[2,5,8,256]{3,2,1,0:T(8,128)S(1)} %get-tuple-element.30) | copy-start | bytes 245764
  1005.2 69.8 %all-reduce.92.cloned.1.call-start = ((), (), s32[]{:S(2)}) async-start(), calls=%async_computation.10 | async-start | bytes 1048576 | tf_op jit(solution)/shard_map/psum | solution.py:274
  1041.4 71.8 %all-reduce.94.cloned.1.call-start = ((), (), s32[]{:S(2)}) async-start(), calls=%async_computation.11 | async-start | bytes 1048576 | tf_op jit(solution)/shard_map/psum | solution.py:274
  1079.5 71.8 %all-reduce.96.cloned.1.call-start = ((), (), s32[]{:S(2)}) async-start(), calls=%async_computation.12 | async-start | bytes 1048576 | tf_op jit(solution)/shard_map/psum | solution.py:274
  1117.6 71.9 %all-reduce.98.cloned.1.call-start = ((), (), s32[]{:S(2)}) async-start(), calls=%async_computation.13 | async-start | bytes 1048576 | tf_op jit(solution)/shard_map/psum | solution.py:274
  1193.2 12.9 %all-to-all-start.1 = ((f32[2,64,256]{2,0,1:T(2,128)}), f32[2,64,256]{2,0,1:T(2,128)S(1)}, u32[]{:S(2)}, u32[]{:S(2)}) async-start(f32[2,64,256]{2,0,1:T(2,128)} %copy.325), calls=%async_computation.2 | async-start | bytes 262144 | tf_op jit(solution)/shard_map/all_to_all | solution.py:277
  (202 other events, 1189.8 us)
Sparse Core Ops, SparseCore 0:
  14.1 123.5 all-reduce.99
  140.6 58.7 all-gather.1
  227.1 32.1 all-reduce.81
  310.5 33.6 all-reduce.83
  434.5 33.4 all-reduce.85
  569.3 33.5 all-reduce.87
  643.6 120.9 all-reduce.101
  766.8 141.6 reduce-scatter.1
  1005.4 31.5 all-reduce.89
  1041.5 33.4 all-reduce.91
  1079.6 33.5 all-reduce.93
  1117.8 33.5 all-reduce.95
  1156.0 33.4 all-reduce.97
where the time goes:
time: 1220 us; the launch traced here: 1210 us
  waiting for transfers between devices  719 us (59%)
  matrix products  250 us (20%)
  blocking collectives  117 us (10%)
  local copies, waits for them, and re-layouts  57.1 us (5%)
  other arithmetic  42.7 us (4%)
  between operations  22.1 us (2%)
    unnamed x15, waiting for transfers between devices  244 us
    psum x5, waiting for transfers between devices, gram_of(): lax.psum(jnp.einsum('krc,krd->kcd', current, current, precision=HIGH), 'p...  166 us
    reduce_scatter x1, waiting for transfers between devices, local(): lax.psum_scatter(grad_muon, ('mesh', 'pts'), scatter_dimension=2, tiled=T...  143 us
    dot_general x38, matrix products, matmul(): return jnp.dot(left, right, precision=HIGH)  86.7 us
    psum x2, waiting for transfers between devices, local(): numerator, denominator = lax.psum((numerator, denominator), 'pts')  62 us
    dot_general x6, matrix products, out_piece(): jnp.einsum('pmhs,mhsd->phd', spread_wts, mixed, precision=HIGH)  54.7 us
    psum x2, waiting for transfers between devices, local(): grad_mixed = lax.psum(grad_mixed, 'pts')  54.3 us
    all_gather x1, waiting for transfers between devices, local(): lax.all_gather(muon_weight, ('mesh', 'pts'), axis=2, tiled=True)  45.1 us
  transfers between devices with their start and end apart: 14, of which 14 were waited for; matrix products, arithmetic and copies ran while one was open for 3% of the time, Pallas kernels for 0%

commit v1 on v0

--- a/solution.py
+++ b/solution.py
@@ -4,6 +4,8 @@
 import jax
 import jax.numpy as jnp
 from jax import lax
+from jax.experimental import pallas as pl
+from jax.experimental.pallas import tpu as pltpu
 from jax.sharding import PartitionSpec as P
 
 C = 256
@@ -15,7 +17,7 @@
 L = 2
 
 
-HIGH = lax.Precision.HIGHEST
+HIGH = lax.Precision.HIGH
 ns_a = 3.4445
 ns_b = -4.775
 ns_c = 2.0315
@@ -179,6 +181,475 @@
     return (new_muon, moment, new_adam, first, second, norm_value)
 
 
+MESH = pl.DeviceIdType.MESH
+SLAB = (8, 256)
+
+
+def grid_of(mesh_count, pts_count):
+    cores = 2 if pts_count % 2 == 0 else 1
+    rows = max(math.isqrt(mesh_count // 2), 1)
+    while mesh_count % rows:
+        rows -= 1
+    return mesh_count // rows, rows, pts_count // cores, cores
+
+
+def place_of(dims):
+    planes, rows, columns, cores = dims
+    across, along = lax.axis_index("mesh"), lax.axis_index("pts")
+    return across // rows, across % rows, along // cores, along % cores
+
+
+def device_at(dims, spot):
+    z, y, x, c = spot
+    return {"mesh": z * dims[1] + y, "pts": x * dims[3] + c}
+
+
+def line_partners(dims, spot):
+    found = []
+    for axis in range(4):
+        for step in range(1, dims[axis]):
+            other = list(spot)
+            other[axis] = lax.rem(spot[axis] + step, dims[axis])
+            found.append(device_at(dims, other))
+    return found
+
+
+def greet(partners):
+    barrier = pltpu.get_barrier_semaphore()
+    for partner in partners:
+        pl.semaphore_signal(barrier, inc=1, device_id=partner, device_id_type=MESH)
+    pl.semaphore_wait(barrier, len(partners))
+
+
+class Mail:
+    def __init__(self, send_sems, recv_sems):
+        self.send_sems, self.recv_sems, self.used, self.open = send_sems, recv_sems, 0, []
+
+    def send(self, source, target, device):
+        copy = pltpu.make_async_remote_copy(
+            src_ref=source,
+            dst_ref=target,
+            send_sem=self.send_sems.at[self.used],
+            recv_sem=self.recv_sems.at[self.used],
+            device_id=device,
+            device_id_type=MESH,
+        )
+        copy.start()
+        self.used += 1
+        self.open.append(copy)
+        return copy
+
+    def close(self):
+        for copy in self.open:
+            copy.wait_send()
+
+
+def gather_kernel(dims, a_in, b_in, c_in, a_all, b_all, c_all, keep, send_sems, recv_sems):
+    planes, rows, columns, cores = dims
+    z, y, x, c = spot = place_of(dims)
+    own = []
+    for index, (source, target) in enumerate(
+        ((a_in, a_all.at[c, x, y, z]), (b_in, b_all.at[c, y, x, z]), (c_in, c_all.at[c, x, y, z]))
+    ):
+        copy = pltpu.make_async_copy(source, target, keep.at[index])
+        copy.start()
+        own.append(copy)
+    greet(line_partners(dims, spot))
+    mail = Mail(send_sems, recv_sems)
+    waits = []
+    for step in range(1, planes):
+        device = device_at(dims, (lax.rem(z + step, planes), y, x, c))
+        waits.append(mail.send(a_in, a_all.at[c, x, y, z], device))
+        waits.append(mail.send(b_in, b_all.at[c, y, x, z], device))
+        waits.append(mail.send(c_in, c_all.at[c, x, y, z], device))
+    for copy in own:
+        copy.wait()
+    for copy in waits:
+        copy.wait_recv()
+    partner = [device_at(dims, (z, y, x, lax.rem(c + step, cores))) for step in range(1, cores)]
+    last = []
+
+    def share(reference):
+        for device in partner:
+            last.append(mail.send(reference, reference, device))
+
+    waits = []
+    for step in range(1, rows):
+        device = device_at(dims, (z, lax.rem(y + step, rows), x, c))
+        for full in (a_all, c_all):
+            waits.append(mail.send(full.at[c, x, y], full.at[c, x, y], device))
+    for step in range(1, columns):
+        device = device_at(dims, (z, y, lax.rem(x + step, columns), c))
+        waits.append(mail.send(b_all.at[c, y, x], b_all.at[c, y, x], device))
+    for reference in (a_all.at[c, x, y], b_all.at[c, y, x], c_all.at[c, x, y]):
+        share(reference)
+    for copy in waits:
+        copy.wait_recv()
+    waits = []
+    for step in range(1, columns):
+        device = device_at(dims, (z, y, lax.rem(x + step, columns), c))
+        for full in (a_all, c_all):
+            waits.append(mail.send(full.at[c, x], full.at[c, x], device))
+    for step in range(1, rows):
+        device = device_at(dims, (z, lax.rem(y + step, rows), x, c))
+        waits.append(mail.send(b_all.at[c, y], b_all.at[c, y], device))
+    for step in range(1, rows):
+        other = lax.rem(y + step, rows)
+        share(a_all.at[c, x, other])
+        share(c_all.at[c, x, other])
+    for step in range(1, columns):
+        share(b_all.at[c, y, lax.rem(x + step, columns)])
+    for copy in waits:
+        copy.wait_recv()
+    for step in range(1, columns):
+        other = lax.rem(x + step, columns)
+        share(a_all.at[c, other])
+        share(c_all.at[c, other])
+    for step in range(1, rows):
+        share(b_all.at[c, lax.rem(y + step, rows)])
+    for copy in last:
+        copy.wait_recv()
+    mail.close()
+
+
+def gather_all(dims, first, second, vector):
+    planes, rows, columns, cores = dims
+    copies = 3 * (planes - 1) + 3 * (rows - 1) + 3 * (columns - 1)
+    copies += (cores - 1) * (3 + 3 * (rows - 1) + 3 * (columns - 1) + 1) + 8
+    shapes = (
+        (cores, columns, rows, planes) + first.shape,
+        (cores, rows, columns, planes) + second.shape,
+        (cores, columns, rows, planes) + vector.shape,
+    )
+    return pl.pallas_call(
+        partial(gather_kernel, dims),
+        out_shape=[jax.ShapeDtypeStruct(shape, jnp.float32) for shape in shapes],
+        in_specs=[pl.BlockSpec(memory_space=pltpu.VMEM)] * 3,
+        out_specs=[pl.BlockSpec(memory_space=pltpu.VMEM)] * 3,
+        scratch_shapes=[
+            pltpu.SemaphoreType.DMA((3,)),
+            pltpu.SemaphoreType.DMA((copies,)),
+            pltpu.SemaphoreType.DMA((copies,)),
+        ],
+        compiler_params=pltpu.CompilerParams(collective_id=0, has_side_effects=True),
+        name="gather_weights",
+    )(first, second, vector)
+
+
+def split3(value):
+    high = value.astype(jnp.bfloat16)
+    return high, (value - high.astype(jnp.float32)).astype(jnp.bfloat16)
+
+
+def dot3(left, right, dims=((1,), (0,))):
+    def one(a, b):
+        return lax.dot_general(a, b, (dims, ((), ())), preferred_element_type=jnp.float32)
+    return one(left[0], right[0]) + (one(left[0], right[1]) + one(left[1], right[0]))
+
+
+def tail_kernel(
+    dims, owners,
+    a_part, b_part, c_part, loss_ref, rate_ref, muon_w, muon_m, adam_w, adam_1, adam_2,
+    new_w, new_m, new_a, new_1, new_2, scal_ref,
+    a1, b1, c1, a2, b2, c2, a3, b3, c3, a4, b4, c4,
+    ga, gb, gc, stat_out, stat_all, g_all, m_all, x_out, x_all,
+    own_sems, send_sems, recv_sems, row_send, row_recv, x_send, x_recv, stat_send, stat_recv,
+):
+    planes, rows, columns, cores = dims
+    z, y, x, c = spot = place_of(dims)
+    mesh_count, pts_count = planes * rows, columns * cores
+    count = mesh_count * pts_count
+    me = lax.axis_index("mesh") * pts_count + lax.axis_index("pts")
+
+    def device_of(number):
+        return {"mesh": number // pts_count, "pts": lax.rem(number, pts_count)}
+
+    barrier = pltpu.get_barrier_semaphore()
+
+    @pl.loop(1, count)
+    def _(step):
+        pl.semaphore_signal(
+            barrier, inc=1, device_id=device_of(lax.rem(me + step, count)), device_id_type=MESH
+        )
+
+    pl.semaphore_wait(barrier, count - 1)
+    mats = len(owners)
+    per = mats // 2
+    def to_owner(k, source, table, slot):
+        return pltpu.make_async_remote_copy(
+            src_ref=source,
+            dst_ref=table.at[me],
+            send_sem=row_send.at[slot],
+            recv_sem=row_recv.at[slot, me],
+            device_id=device_of(owners[k]),
+            device_id_type=MESH,
+        )
+
+    for k in range(mats):
+        @pl.when(me != owners[k])
+        def _():
+            to_owner(k, muon_m.at[k], m_all, k).start()
+
+        @pl.when(me == owners[k])
+        def _():
+            m_all[me] = muon_m[k]
+
+    mail = Mail(send_sems, recv_sems)
+    waits = []
+    for step in range(1, cores):
+        other = lax.rem(c + step, cores)
+        device = device_at(dims, (z, y, x, other))
+        for part, landing in ((a_part, a1), (b_part, b1), (c_part, c1)):
+            waits.append(mail.send(part.at[other], landing.at[step - 1], device))
+    for copy in waits:
+        copy.wait_recv()
+    for part, landing in ((a_part, a1), (b_part, b1), (c_part, c1)):
+        total = part[c]
+        for step in range(cores - 1):
+            total = total + landing[step]
+        landing[0] = total
+    waits = []
+    for step in range(1, columns):
+        other = lax.rem(x + step, columns)
+        device = device_at(dims, (z, y, other, c))
+        waits.append(mail.send(a1.at[0, other], a2.at[step - 1], device))
+        waits.append(mail.send(c1.at[0, other], c2.at[step - 1], device))
+    for step in range(1, rows):
+        other = lax.rem(y + step, rows)
+        device = device_at(dims, (z, other, x, c))
+        waits.append(mail.send(b1.at[0, other], b2.at[step - 1], device))
+    for copy in waits:
+        copy.wait_recv()
+    for full, landing, at, extent in (
+        (a1, a2, x, columns), (b1, b2, y, rows), (c1, c2, x, columns),
+    ):
+        total = full[0, at]
+        for step in range(extent - 1):
+            total = total + landing[step]
+        landing[0] = total
+    waits = []
+    for step in range(1, rows):
+        other = lax.rem(y + step, rows)
+        device = device_at(dims, (z, other, x, c))
+        waits.append(mail.send(a2.at[0, other], a3.at[step - 1], device))
+        waits.append(mail.send(c2.at[0, other], c3.at[step - 1], device))
+    for step in range(1, columns):
+        other = lax.rem(x + step, columns)
+        device = device_at(dims, (z, y, other, c))
+        waits.append(mail.send(b2.at[0, other], b3.at[step - 1], device))
+    for copy in waits:
+        copy.wait_recv()
+    for full, landing, at, extent in (
+        (a2, a3, y, rows), (b2, b3, x, columns), (c2, c3, y, rows),
+    ):
+        total = full[0, at]
+        for step in range(extent - 1):
+            total = total + landing[step]
+        landing[0] = total
+    waits = []
+    for step in range(1, planes):
+        other = lax.rem(z + step, planes)
+        device = device_at(dims, (other, y, x, c))
+        for full, landing in ((a3, a4), (b3, b4), (c3, c4)):
+            waits.append(mail.send(full.at[0, other], landing.at[step - 1], device))
+    for copy in waits:
+        copy.wait_recv()
+    for full, landing, final in ((a3, a4, ga), (b3, b4, gb), (c3, c4, gc)):
+        total = full[0, z]
+        for step in range(planes - 1):
+            total = total + landing[step]
+        final[...] = total
+
+    for k in range(mats):
+        source = ga if k < per else gb
+
+        @pl.when(me != owners[k])
+        def _():
+            to_owner(k, source.at[k % per], g_all, mats + k).start()
+
+        @pl.when(me == owners[k])
+        def _():
+            g_all[me] = source[k % per]
+
+    squares = jnp.sum(ga[...] * ga[...], axis=0) + jnp.sum(gb[...] * gb[...], axis=0)
+    squares = squares + jnp.sum(gc[...] * gc[...], axis=0)
+    square = jnp.sum(squares)
+    lane = lax.broadcasted_iota(jnp.int32, (1, 128), 1)
+    stat_out[...] = jnp.where(lane == 0, square, jnp.where(lane == 1, loss_ref[0], 0.0))
+    stat_all[me] = stat_out[...]
+
+    def stat_copy(step):
+        return pltpu.make_async_remote_copy(
+            src_ref=stat_out,
+            dst_ref=stat_all.at[me],
+            send_sem=stat_send.at[step],
+            recv_sem=stat_recv.at[step],
+            device_id=device_of(lax.rem(me + step, count)),
+            device_id_type=MESH,
+        )
+
+    @pl.loop(1, count)
+    def _(step):
+        stat_copy(step).start()
+
+    @pl.loop(1, count)
+    def _(step):
+        stat_copy(step).wait_recv()
+
+    stats = jnp.sum(stat_all[...], axis=0)
+    square_sum = jnp.sum(jnp.where(lane == 0, stats, 0.0))
+    loss_sum = jnp.sum(jnp.where(lane == 1, stats, 0.0))
+    norm = jnp.sqrt(jnp.full((8, 256), square_sum, jnp.float32))
+    factor = 0.1 / jnp.maximum(norm, 0.1)
+    row = lax.broadcasted_iota(jnp.int32, (8, 128), 0)
+    scal_ref[...] = jnp.where(row == 0, norm[:, :128], jnp.full((8, 128), loss_sum, jnp.float32))
+
+    for k in range(mats):
+        @pl.when(me == owners[k])
+        def _():
+            for slot in (k, mats + k):
+                table = m_all if slot < mats else g_all
+
+                @pl.loop(1, count)
+                def _(step):
+                    source = lax.rem(me + step, count)
+                    pltpu.make_async_remote_copy(
+                        src_ref=muon_m.at[k],
+                        dst_ref=table.at[source],
+                        send_sem=row_send.at[slot],
+                        recv_sem=row_recv.at[slot, source],
+                        device_id=device_of(source),
+                        device_id_type=MESH,
+                    ).wait_recv()
+
+            moment = 0.95 * m_all[...] + factor[None] * g_all[...]
+            moment = moment.reshape(count * moment.shape[1], moment.shape[2])
+            frob = jnp.sum(moment * moment)
+            scale = jnp.sqrt(jnp.full((8, 256), frob, jnp.float32)) + 1e-07
+            current = moment / scale[:1]
+            for sweep in range(5):
+                pair = split3(current)
+                gram = split3(dot3(pair, pair, ((0,), (0,))))
+                product = dot3(pair, gram)
+                current = (
+                    ns_a * current + ns_b * product + ns_c * dot3(split3(product), gram)
+                )
+            x_out[...] = current.reshape(x_out.shape)
+            x_all[k] = x_out[me]
+
+            @pl.loop(1, count)
+            def _(step):
+                target = lax.rem(me + step, count)
+                pltpu.make_async_remote_copy(
+                    src_ref=x_out.at[target],
+                    dst_ref=x_all.at[k],
+                    send_sem=x_send.at[target],
+                    recv_sem=x_recv.at[k],
+                    device_id=device_of(target),
+                    device_id_type=MESH,
+                ).start()
+
+    new_m[:per] = 0.95 * muon_m[:per] + factor[None] * ga[...]
+    new_m[per:] = 0.95 * muon_m[per:] + factor[None] * gb[...]
+    rate, keep1, keep2 = rate_ref[0], rate_ref[1], rate_ref[2]
+    clipped = factor[None] * gc[...]
+    first = 0.9 * adam_1[...] + 0.1 * clipped
+    second = 0.999 * adam_2[...] + 0.001 * clipped * clipped
+    new_1[...] = first
+    new_2[...] = second
+    first_hat = first / keep1
+    second_hat = second / keep2
+    new_a[...] = adam_w[...] * (1.0 - rate * 0.01) - rate * first_hat / (
+        jnp.sqrt(second_hat) + 1e-08
+    )
+    for k in range(mats):
+        @pl.when(me != owners[k])
+        def _():
+            pltpu.make_async_remote_copy(
+                src_ref=x_out.at[me],
+                dst_ref=x_all.at[k],
+                send_sem=x_send.at[me],
+                recv_sem=x_recv.at[k],
+                device_id=device_of(owners[k]),
+                device_id_type=MESH,
+            ).wait_recv()
+
+    new_w[...] = muon_w[...] * (1.0 - rate * 0.01) - rate * (0.2 * C**0.5) * x_all[...]
+    mail.close()
+
+    @pl.loop(1, count)
+    def _(step):
+        stat_copy(step).wait_send()
+
+    for k in range(mats):
+        @pl.when(me != owners[k])
+        def _():
+            to_owner(k, muon_m.at[k], m_all, k).wait_send()
+            to_owner(k, ga.at[k % per], g_all, mats + k).wait_send()
+
+        @pl.when(me == owners[k])
+        def _():
+            @pl.loop(1, count)
+            def _(step):
+                target = lax.rem(me + step, count)
+                pltpu.make_async_remote_copy(
+                    src_ref=x_out.at[target],
+                    dst_ref=x_all.at[k],
+                    send_sem=x_send.at[target],
+                    recv_sem=x_recv.at[k],
+                    device_id=device_of(target),
+                    device_id_type=MESH,
+                ).wait_send()
+
+
+def tail_update(dims, first, second, vector, loss, rates, muon_w, muon_m, adam_w, adam_1, adam_2):
+    planes, rows, columns, cores = dims
+    count = planes * rows * columns * cores
+    mats = muon_m.shape[0]
+    owners = tuple(k * count // mats for k in range(mats))
+    blocks = (first.shape[4:], second.shape[4:], vector.shape[4:])
+    orders = ((columns, rows, planes), (rows, columns, planes), (columns, rows, planes))
+    landings = []
+    for stage in range(4):
+        for block, order, extents in zip(
+            blocks, orders,
+            ((cores, columns, rows, planes), (cores, rows, columns, planes), (cores, columns, rows, planes)),
+        ):
+            lead = max(extents[stage] - 1, 1)
+            landings.append(pltpu.VMEM((lead,) + order[stage:] + block, jnp.float32))
+    copies = 3 * (planes + rows + columns + cores)
+    vmem = pl.BlockSpec(memory_space=pltpu.VMEM)
+    smem = pl.BlockSpec(memory_space=pltpu.SMEM)
+    dma = pltpu.SemaphoreType.DMA
+    out = [muon_w, muon_m, adam_w, adam_1, adam_2]
+    return pl.pallas_call(
+        partial(tail_kernel, dims, owners),
+        out_shape=[jax.ShapeDtypeStruct(item.shape, jnp.float32) for item in out]
+        + [jax.ShapeDtypeStruct((8, 128), jnp.float32)],
+        in_specs=[vmem] * 3 + [smem] * 2 + [vmem] * 5,
+        out_specs=[vmem] * 6,
+        scratch_shapes=landings
+        + [
+            pltpu.VMEM(blocks[0], jnp.float32),
+            pltpu.VMEM(blocks[1], jnp.float32),
+            pltpu.VMEM(blocks[2], jnp.float32),
+            pltpu.VMEM((1, 128), jnp.float32),
+            pltpu.VMEM((count, 1, 128), jnp.float32),
+            pltpu.VMEM((count,) + muon_m.shape[1:], jnp.float32),
+            pltpu.VMEM((count,) + muon_m.shape[1:], jnp.float32),
+            pltpu.VMEM((count,) + muon_m.shape[1:], jnp.float32),
+            pltpu.VMEM(muon_m.shape, jnp.float32),
+            dma((1,)), dma((copies,)), dma((copies,)),
+            dma((2 * mats,)), dma((2 * mats, count)), dma((count,)), dma((mats,)),
+            dma((count,)), dma((count,)),
+        ],
+        compiler_params=pltpu.CompilerParams(
+            collective_id=1, has_side_effects=True, vmem_limit_bytes=60 * 1024 * 1024
+        ),
+        name="reduce_and_update",
+    )(first, second, vector, loss, rates, muon_w, muon_m, adam_w, adam_1, adam_2)
+
+
 def local(
     inputs,
     target,
@@ -293,6 +764,133 @@
     return (results[0], results[1], results[2], results[3], results[4], loss_total, results[5])
 
 
+def local_fast(
+    inputs,
+    target,
+    lengths,
+    step_count,
+    muon_weight,
+    muon_moment,
+    adam_weight,
+    adam_first,
+    adam_second,
+):
+    mesh_count, pts_count = lax.axis_size("mesh"), lax.axis_size("pts")
+    dims = grid_of(mesh_count, pts_count)
+    planes, rows, columns, cores = dims
+    count = mesh_count * pts_count
+    shard, span = adam_weight.shape[0], muon_weight.shape[2]
+    mats = muon_weight.shape[0] * muon_weight.shape[1]
+    slabs = span // 8
+    pad = -(-shard // 2048) * 2048
+
+    def slab_of(vector):
+        return jnp.pad(vector, (0, pad - shard)).reshape(-1, 8, 256)
+
+    def stacked(value):
+        return value.reshape(mats * slabs, 8, 256)
+
+    half = muon_weight.shape[1] * slabs
+    all_first, all_second, all_vector = gather_all(
+        dims, muon_weight[0].reshape(half, 8, 256), muon_weight[1].reshape(half, 8, 256), slab_of(adam_weight)
+    )
+
+    def matrices_of(value, order):
+        value = value.reshape(value.shape[:4] + (half // slabs, slabs, 8, 256))
+        value = jnp.transpose(value, (4,) + order + (5, 6, 7))
+        return value.reshape(half // slabs, count * span, 256)
+
+    muon_all = (
+        matrices_of(all_first, (3, 2, 1, 0)), matrices_of(all_second, (3, 1, 2, 0))
+    )
+    adam_all = jnp.transpose(all_vector, (3, 2, 1, 0, 4, 5, 6)).reshape(count, pad)[:, :shard].reshape(-1)
+    points = inputs.shape[0]
+    pts_count = lax.axis_size("pts")
+    floor_value = float(points * pts_count)
+    onehot = mesh_mask(lengths[0], lax.axis_index("pts") * points, points)
+    meshes = lax.axis_size("mesh") * lengths.shape[1]
+    hidden, embed_back = jax.vjp(lambda packed: embed_piece(inputs, packed), adam_all)
+    saved = []
+    for layer_index in range(L):
+        matrices = muon_all[layer_index]
+        (weights, numerator, denominator), slice_back = jax.vjp(
+            partial(slice_piece, layer_index=layer_index, onehot=onehot), hidden, matrices, adam_all
+        )
+        numerator, denominator = lax.psum((numerator, denominator), "pts")
+        mixed, mix_back = jax.vjp(
+            partial(mix_piece, layer_index=layer_index), numerator, denominator, adam_all
+        )
+        following, out_back = jax.vjp(
+            partial(out_piece, layer_index=layer_index, onehot=onehot),
+            hidden,
+            weights,
+            mixed,
+            matrices,
+            adam_all,
+        )
+        saved.append((slice_back, mix_back, out_back))
+        hidden = following
+    (errors, scales), head_back = jax.vjp(
+        lambda state, packed: head_piece(state, packed, target, onehot), hidden, adam_all
+    )
+    errors, scales = lax.psum((errors, scales), "pts")
+    group_loss, loss_back = jax.vjp(
+        lambda first, second: loss_piece(first, second, meshes, floor_value), errors, scales
+    )
+    grad_errors, grad_scales = loss_back(jnp.ones_like(group_loss))
+    grad_hidden, grad_adam = head_back((grad_errors, grad_scales))
+    grad_layers = [None] * L
+    for layer_index in reversed(range(L)):
+        slice_back, mix_back, out_back = saved[layer_index]
+        grad_hidden_out, grad_weights, grad_mixed, grad_mats_out, grad_adam_out = out_back(
+            grad_hidden
+        )
+        grad_mixed = lax.psum(grad_mixed, "pts")
+        grad_num, grad_den, grad_adam_mix = mix_back(grad_mixed)
+        grad_hidden_in, grad_mats_in, grad_adam_in = slice_back((grad_weights, grad_num, grad_den))
+        grad_hidden = grad_hidden_out + grad_hidden_in
+        grad_adam = grad_adam + grad_adam_out + grad_adam_in + grad_adam_mix / pts_count
+        grad_layers[layer_index] = grad_mats_out + grad_mats_in
+    (grad_embed,) = embed_back(grad_hidden)
+    grad_adam = grad_adam + grad_embed
+    def parts_of(value, order):
+        value = value.reshape(half // slabs, planes, rows, columns, cores, slabs, 8, 256)
+        value = jnp.transpose(value, order + (0, 5, 6, 7))
+        return value.reshape(value.shape[:4] + (half, 8, 256))
+
+    adam_parts = jnp.pad(grad_adam.reshape(count, shard), ((0, 0), (0, pad - shard)))
+    adam_parts = adam_parts.reshape(planes, rows, columns, cores, -1, 8, 256)
+    adam_parts = jnp.transpose(adam_parts, (3, 2, 1, 0, 4, 5, 6))
+    step = step_count[0].astype(jnp.float32)
+    rates = jnp.stack([one_cycle(step), 1.0 - 0.9**step, 1.0 - 0.999**step])
+    results = tail_update(
+        dims,
+        parts_of(grad_layers[0], (4, 3, 2, 1)),
+        parts_of(grad_layers[1], (4, 2, 3, 1)),
+        adam_parts,
+        jnp.reshape(group_loss / pts_count, (1,)),
+        rates,
+        stacked(muon_weight),
+        stacked(muon_moment),
+        slab_of(adam_weight),
+        slab_of(adam_first),
+        slab_of(adam_second),
+    )
+
+    def unslab(value):
+        return value.reshape(-1)[:shard]
+
+    return (
+        results[0].reshape(muon_weight.shape),
+        results[1].reshape(muon_weight.shape),
+        unslab(results[2]),
+        unslab(results[3]),
+        unslab(results[4]),
+        results[5][1, 0],
+        results[5][0, 0],
+    )
+
+
 def solution(mesh):
     in_specs = (
         P(("mesh", "pts"), None),
@@ -314,4 +912,7 @@
         P(),
         P(),
     )
-    return jax.shard_map(local, mesh=mesh, in_specs=in_specs, out_specs=out_specs, check_vma=False)
+    def chosen(*args):
+        return (local_fast if args[4].shape[2] == 8 else local)(*args)
+
+    return jax.shard_map(chosen, mesh=mesh, in_specs=in_specs, out_specs=out_specs, check_vma=False)

time: 1220 us -> 532 us (0.44)
  waiting for transfers between devices: 719 us -> 86.6 us
  matrix products: 250 us -> 145 us
  Pallas kernels: 0 us -> 99.3 us
  blocking collectives: 117 us -> 29.4 us
  local copies, waits for them, and re-layouts: 57.1 us -> 94 us
    unnamed x15 -> x4, waiting for transfers between devices: 244 us -> 0.07 us
    psum x9 -> x4, waiting for transfers between devices: 282 us -> 86.5 us  [the longest x2 54.6 us: local_fast(): grad_mixed = lax.psum(grad_mixed, 'pts')]
    reduce_scatter x1 -> x0, waiting for transfers between devices: 143 us -> none  [local(): lax.psum_scatter(grad_muon, ('mesh', 'pts'), scatter_dimension=2, tiled=T...]
    pallas_call x0 -> x2, Pallas kernels: none -> 99.3 us  [the longest x1 67 us: tail_update(): pl.pallas_call(partial(tail_kernel, dims, owners), out_shape=[jax.ShapeDt...]
    psum x5 -> x3, blocking collectives: 105 us -> 29.4 us  [the longest x2 23 us: local_fast(): numerator, denominator = lax.psum((numerator, denominator), 'pts')]
    all_gather x1 -> x0, waiting for transfers between devices: 45.1 us -> none  [local(): lax.all_gather(muon_weight, ('mesh', 'pts'), axis=2, tiled=True)]
    dot_general x38, matrix products: 86.7 us -> 56.9 us  [matmul(): return jnp.dot(left, right, precision=HIGH)]
    dot_general x6, matrix products: 54.7 us -> 31.7 us  [out_piece(): jnp.einsum('pmhs,mhsd->phd', spread_wts, mixed, precision=HIGH)]
  transfers between devices with their start and end apart: 14 -> 4, of which waited for: 14 -> 3; matrix products, arithmetic and copies ran while one was open for 3% -> 11% of each run, Pallas kernels for 0% -> 0%
where the time goes in v1:
time: 532 us; the launch traced here: 527 us
  matrix products  145 us (27%)
  Pallas kernels  99.3 us (19%)
  local copies, waits for them, and re-layouts  94 us (18%)
  waiting for transfers between devices  86.6 us (16%)
  other arithmetic  54.2 us (10%)
  blocking collectives  29.4 us (6%)
  between operations  18.8 us (4%)
    pallas_call x1, Pallas kernels, tail_update(): pl.pallas_call(partial(tail_kernel, dims, owners), out_shape=[jax.ShapeDt...  67 us
    dot_general x38, matrix products, matmul(): return jnp.dot(left, right, precision=HIGH)  56.9 us
    psum x2, waiting for transfers between devices, local_fast(): grad_mixed = lax.psum(grad_mixed, 'pts')  54.6 us
    pallas_call x1, Pallas kernels, gather_all(): pl.pallas_call(partial(gather_kernel, dims), out_shape=[jax.ShapeDtypeStr...  32.3 us
    psum x2, waiting for transfers between devices, local_fast(): numerator, denominator = lax.psum((numerator, denominator), 'pts')  32 us
    dot_general x6, matrix products, out_piece(): jnp.einsum('pmhs,mhsd->phd', spread_wts, mixed, precision=HIGH)  31.7 us
    psum x2, blocking collectives, local_fast(): numerator, denominator = lax.psum((numerator, denominator), 'pts')  23 us
    unnamed x535, local copies, waits for them, and re-layouts  22.1 us
  transfers between devices with their start and end apart: 4, of which 3 were waited for; matrix products, arithmetic and copies ran while one was open for 11% of the time, Pallas kernels for 0%

profile of v1, /device:TPU:0, one launch (start us, length us, event | category | flops | bytes accessed | tf_op | source)
XLA Modules:
  0.0 527.5 jit_solution(16368094022967680376)
XLA Ops:
  10.0 32.3 %gather_weights.1 = (f32[2,2,2,4,5,8,256]{6,5,4,3,2,1,0:T(8,128)}, f32[2,2,2,4,5,8,256]{6,5,4,3,2,1,0:T(8,128)}, f32[2,2,2,4,1,8,256]{6,5,4,3,2,1,0:T(8,128)}) custom-call(f32[5,8,256]{2,1,0:T(8,128)} %get-tuple-element.70.a_in, f32[5,8,256]{2,1,0:T(8,128)} %get-tuple-element.69.b_in, f32[1,8,256]{2,1,0:T(8,128)} %reshape.726.c_in.adam_w), custom_call_target="tpu_custom_call" | custom-call | tf_op jit(solution)/shard_map/gather_weights/pallas_call | solution.py:324
  56.9 2.7 fusion.42
  68.2 11.8 %psum.57 = f32[4,8,64]{2,1,0:T(8,128)} all-reduce(f32[4,8,64]{2,1,0:T(8,128)} %copy.226), channel_id=1, replica_groups=mesh['mesh'=8,'pts'=4] {'pts'}, use_global_device_ids=true, to_apply=%region_6.7 | all-reduce | flops 2048 | bytes 16384 | tf_op jit(solution)/shard_map/psum | solution.py:819
  99.3 2.5 slice.313
  126.4 2.7 fusion.2
  130.3 3.1 fusion.53
  134.7 12.3 %multiply_reduce_fusion.20 = f32[1024]{0:T(1024)S(1)} fusion(f32[1024,256]{0,1:T(8,128)S(1)} %get-tuple-element.126, f32[1024]{0:T(1024)S(1)} %broadcast_multiply_fusion.10), kind=kLoop, calls=%fused_computation.159 | loop fusion | flops 785408 | bytes 1056768 | tf_op jit(solution)/shard_map/jvp()/reduce_sum | solution.py:63
  153.3 11.2 %psum.59 = f32[4,8,64]{2,1,0:T(8,128)} all-reduce(f32[4,8,64]{2,1,0:T(8,128)} %copy.241), channel_id=1, replica_groups=mesh['mesh'=8,'pts'=4] {'pts'}, use_global_device_ids=true, to_apply=%region_16.17 | all-reduce | flops 2048 | bytes 16384 | tf_op jit(solution)/shard_map/psum | solution.py:819
  169.9 2.7 fusion.47
  174.0 32.0 %all-reduce.77.cloned.1.call-done = f32[4,8,64,32]{2,3,0,1:T(8,128)} async-done(((f32[4,8,64,32]{2,3,0,1:T(8,128)}), f32[4,8,64,32]{2,3,0,1:T(8,128)}) %all-reduce.77.cloned.1.call-update) | async-done | bytes 262160 | tf_op jit(solution)/shard_map/psum | solution.py:819
  213.7 2.7 fusion
  217.6 3.1 fusion.54
  226.4 6.4 %all-reduce.69 = (f32[4]{0:T(128)}, f32[4]{0:T(128)}) all-reduce(f32[4]{0:T(128)} %convolution_bitcast_fusion.21, f32[4]{0:T(128)} %convolution_bitcast_fusion.22), channel_id=1, replica_groups=mesh['mesh'=8,'pts'=4] {'pts'}, use_global_device_ids=true, to_apply=%region_26.27 | all-reduce | flops 8 | bytes 64 | tf_op jit(solution)/shard_map/psum | solution.py:836
  234.8 3.1 fusion.238
  237.9 2.6 fusion.67
  240.4 2.5 copy.255
  243.0 2.6 multiply_reduce_fusion.11
  252.6 2.2 fusion.236
  254.8 2.5 copy.256
  265.9 6.7 %fusion.40 = f32[4,8,64,32]{2,3,0,1:T(8,128)} fusion(f32[8,32,1024,1]{2,1,3,0:T(8,128)S(1)} %convolution_bitcast_fusion.1, f32[1024,8,64]{0,2,1:T(8,128)S(1)} %copy-done.16, f32[1024,4]{0,1:T(4,128)S(1)} %copy-done.133), kind=kOutput, calls=%fused_computation.84 | convolution fusion | flops 404750336 | bytes 3424256 | tf_op jit(solution)/shard_map/transpose(jvp(pmhs,mhsd->phd))/dot_general | solution.py:109
  272.6 6.6 %multiply_reduce_fusion.1 = f32[8,1024,64]{1,2,0:T(8,128)} fusion(f32[1024,4]{0,1:T(4,128)} %copy-done.129, f32[8,32,1024,1]{2,1,3,0:T(8,128)} %copy-done.77, f32[4,8,64,32]{2,3,1,0:T(8,128)} %copy-done.262), kind=kOutput, calls=%fused_computation.5 | convolution fusion | flops 406323200 | bytes 3424256 | tf_op jit(solution)/shard_map/transpose(jvp(pmhs,mhsd->phd))/dot_general | solution.py:109
  289.3 23.4 %all-reduce.79.cloned.1.call-done = f32[4,8,64,32]{2,3,0,1:T(8,128)} async-done(((f32[4,8,64,32]{2,3,0,1:T(8,128)}), f32[4,8,64,32]{2,3,0,1:T(8,128)}) %all-reduce.79.cloned.1.call-update) | async-done | bytes 262160 | tf_op jit(solution)/shard_map/psum | solution.py:848
  312.8 2.8 multiply_reduce_fusion.15
  321.7 3.0 fusion.13
  335.9 2.8 convolution_bitcast_fusion.2
  347.9 2.1 fusion.234
  356.4 6.7 %fusion.41 = f32[4,8,64,32]{2,3,0,1:T(8,128)} fusion(f32[8,32,1024,1]{2,1,3,0:T(8,128)S(1)} %convolution_bitcast_fusion, f32[1024,8,64]{0,2,1:T(8,128)S(1)} %copy-done.9, f32[1024,4]{0,1:T(4,128)S(1)} %copy-done.135), kind=kOutput, calls=%fused_computation.85 | convolution fusion | flops 404750336 | bytes 3424256 | tf_op jit(solution)/shard_map/transpose(jvp(pmhs,mhsd->phd))/dot_general | solution.py:109
  363.2 6.4 %multiply_reduce_fusion = f32[8,1024,64]{1,2,0:T(8,128)} fusion(f32[1024,4]{0,1:T(4,128)S(1)} %copy-done.135, f32[8,32,1024,1]{2,1,3,0:T(8,128)S(1)} %convolution_bitcast_fusion, f32[4,8,64,32]{2,3,1,0:T(8,128)} %copy-done.261), kind=kOutput, calls=%fused_computation.4 | convolution fusion | flops 406323200 | bytes 3424256 | tf_op jit(solution)/shard_map/transpose(jvp(pmhs,mhsd->phd))/dot_general | solution.py:109
  382.2 2.5 convolution_bitcast_fusion.9
  384.7 31.1 %all-reduce.81.cloned.1.call-done = f32[4,8,64,32]{2,3,0,1:T(8,128)} async-done(((f32[4,8,64,32]{2,3,0,1:T(8,128)}), f32[4,8,64,32]{2,3,0,1:T(8,128)}) %all-reduce.81.cloned.1.call-update) | async-done | bytes 262160 | tf_op jit(solution)/shard_map/psum | solution.py:848
  415.8 2.4 multiply_reduce_fusion.12
  445.5 67.0 %reduce_and_update.1 = (f32[10,8,256]{2,1,0:T(8,128)}, f32[10,8,256]{2,1,0:T(8,128)}, f32[1,8,256]{2,1,0:T(8,128)}, f32[1,8,256]{2,1,0:T(8,128)}, f32[1,8,256]{2,1,0:T(8,128)}, /*index=5*/f32[8,128]{1,0:T(8,128)}) custom-call(f32[2,2,2,4,5,8,256]{6,5,4,3,2,1,0:T(8,128)} %bitcast.434, f32[2,2,2,4,5,8,256]{6,5,4,3,2,1,0:T(8,128)} %bitcast.433, ...), custom_call_target="tpu_custom_call" | custom-call | tf_op jit(solution)/shard_map/reduce_and_update/pallas_call | solution.py:625
  (782 shorter events, 204.3 us)
Async XLA Ops:
  7.2 42.9 %copy-start = (f32[1024,8]{0,1:T(8,128)S(1)}, f32[1024,8]{0,1:T(8,128)}, u32[]{:S(2)}) copy-start(f32[1024,8]{0,1:T(8,128)} %param.9) | copy-start | bytes 98308
  7.2 111.9 %all-reduce.75.cloned.1.call-start = ((), (), s32[]{:S(2)}) async-start(), calls=%async_computation | async-start | bytes 1048576 | tf_op jit(solution)/shard_map/psum | solution.py:819
  44.2 9.0 %copy-start.223 = (f32[64]{0:T(128)}, f32[64]{0:T(128)S(1)}, u32[]{:S(2)}) copy-start(f32[64]{0:T(128)S(1)} %get-tuple-element.101) | copy-start | bytes 772
  44.8 8.3 %copy-start.225 = (f32[8]{0:T(128)}, f32[8]{0:T(128)S(1)}, u32[]{:S(2)}) copy-start(f32[8]{0:T(128)S(1)} %get-tuple-element.74) | copy-start | bytes 100
  55.0 71.3 %copy-start.8 = (f32[1024,8,64]{0,2,1:T(8,128)}, f32[1024,8,64]{0,2,1:T(8,128)S(1)}, u32[]{:S(2)}) copy-start(f32[1024,8,64]{0,2,1:T(8,128)S(1)} %fusion.36) | copy-start | bytes 6291460
  59.6 146.4 %all-reduce.77.cloned.1.call-start = ((), (), s32[]{:S(2)}) async-start(), calls=%async_computation.1 | async-start | bytes 1048576 | tf_op jit(solution)/shard_map/psum | solution.py:819
  104.4 12.1 %copy-start.170 = (f32[4,8,64]{2,1,0:T(8,128)S(1)}, f32[4,8,64]{2,1,0:T(8,128)}, u32[]{:S(2)}) copy-start(f32[4,8,64]{2,1,0:T(8,128)} %get-tuple-element.107) | copy-start | bytes 24580
  104.4 12.7 %copy-start.169 = (f32[4,8,64]{2,1,0:T(8,128)S(1)}, f32[4,8,64]{2,1,0:T(8,128)}, u32[]{:S(2)}) copy-start(f32[4,8,64]{2,1,0:T(8,128)} %get-tuple-element.109) | copy-start | bytes 24580
  104.4 12.7 %copy-start.168 = (f32[8,4,64]{2,0,1:T(8,128)S(1)}, f32[8,4,64]{2,0,1:T(8,128)}, u32[]{:S(2)}) copy-start(f32[8,4,64]{2,0,1:T(8,128)} %get-tuple-element.108) | copy-start | bytes 24580
  104.4 14.7 %copy-start.214 = (f32[32,32]{1,0:T(8,128)S(1)}, f32[32,32]{1,0:T(8,128)}, u32[]{:S(2)}) copy-start(f32[32,32]{1,0:T(8,128)} %squeeze.84) | copy-start | bytes 12292
  107.5 6.8 %copy-start.76 = (f32[1,4,2,2,2,1,8,256]{7,6,0,1,3,2,4,5:T(8,128)S(1)}, f32[1,4,2,2,2,1,8,256]{7,6,0,1,3,2,4,5:T(8,128)}, u32[]{:S(2)}) copy-start(f32[1,4,2,2,2,1,8,256]{7,6,0,1,3,2,4,5:T(8,128)} %get-tuple-element.59) | copy-start | bytes 786436
  107.5 7.5 %copy-start.75 = (f32[1,4,2,2,2,1,8,256]{7,6,0,1,3,2,4,5:T(8,128)S(1)}, f32[1,4,2,2,2,1,8,256]{7,6,0,1,3,2,4,5:T(8,128)}, u32[]{:S(2)}) copy-start(f32[1,4,2,2,2,1,8,256]{7,6,0,1,3,2,4,5:T(8,128)} %get-tuple-element.61) | copy-start | bytes 786436
  107.5 8.3 %copy-start.74 = (f32[1,4,2,2,2,1,8,256]{7,6,0,1,3,2,4,5:T(8,128)S(1)}, f32[1,4,2,2,2,1,8,256]{7,6,0,1,3,2,4,5:T(8,128)}, u32[]{:S(2)}) copy-start(f32[1,4,2,2,2,1,8,256]{7,6,0,1,3,2,4,5:T(8,128)} %get-tuple-element.62) | copy-start | bytes 786436
  112.6 7.9 %copy-start.215 = (f32[32,32]{1,0:T(8,128)S(1)}, f32[32,32]{1,0:T(8,128)}, u32[]{:S(2)}) copy-start(f32[32,32]{1,0:T(8,128)} %squeeze.83) | copy-start | bytes 12292
  133.4 13.7 %copy-start.56 = (f32[1,4,2,2,2,1,8,256]{7,6,4,3,2,1,5,0:T(8,128)S(1)}, f32[1,4,2,2,2,1,8,256]{7,6,4,3,2,1,5,0:T(8,128)}, u32[]{:S(2)}) copy-start(f32[1,4,2,2,2,1,8,256]{7,6,4,3,2,1,5,0:T(8,128)} %copy.240) | copy-start | bytes 786436
  133.4 13.7 %copy-start.171 = (f32[256]{0:T(256)S(1)}, f32[256]{0:T(256)}, u32[]{:S(2)}) copy-start(f32[256]{0:T(256)} %get-tuple-element.85) | copy-start | bytes 3076
  133.4 13.7 %copy-start.192 = (f32[256]{0:T(256)S(1)}, f32[256]{0:T(256)}, u32[]{:S(2)}) copy-start(f32[256]{0:T(256)} %get-tuple-element.84) | copy-start | bytes 3076
  133.5 13.7 %copy-start.232 = (f32[256]{0:T(256)S(1)}, f32[256]{0:T(256)}, u32[]{:S(2)}) copy-start(f32[256]{0:T(256)} %get-tuple-element.82) | copy-start | bytes 3076
  134.7 13.2 %copy-start.162 = (f32[32,64,1]{1,0,2:T(8,128)S(1)}, f32[32,64,1]{1,0,2:T(8,128)}, u32[]{:S(2)}) copy-start(f32[32,64,1]{1,0,2:T(8,128)} %reshape.814) | copy-start | bytes 24580
  134.7 13.2 %copy-start.227 = (f32[64]{0:T(128)S(1)}, f32[64]{0:T(128)}, u32[]{:S(2)}) copy-start(f32[64]{0:T(128)} %get-tuple-element.100) | copy-start | bytes 772
  134.7 13.3 %copy-start.229 = (f32[8]{0:T(128)S(1)}, f32[8]{0:T(128)}, u32[]{:S(2)}) copy-start(f32[8]{0:T(128)} %get-tuple-element.73) | copy-start | bytes 100
  172.7 140.1 %all-reduce.79.cloned.1.call-start = ((), (), s32[]{:S(2)}) async-start(), calls=%async_computation.2 | async-start | bytes 1048576 | tf_op jit(solution)/shard_map/psum | solution.py:848
  210.6 15.1 %copy-start.165 = (f32[4,8,64]{2,1,0:T(8,128)}, f32[4,8,64]{2,1,0:T(8,128)S(1)}, u32[]{:S(2)}) copy-start(f32[4,8,64]{2,1,0:T(8,128)S(1)} %fusion.82) | copy-start | bytes 24580
  279.2 136.7 %all-reduce.81.cloned.1.call-start = ((), (), s32[]{:S(2)}) async-start(), calls=%async_computation.3 | async-start | bytes 1048576 | tf_op jit(solution)/shard_map/psum | solution.py:848
  371.4 7.7 %copy-start.64 = (f32[1,256,256]{2,1,0:T(8,128)S(1)}, f32[1,256,256]{2,1,0:T(8,128)}, u32[]{:S(2)}) copy-start(f32[1,256,256]{2,1,0:T(8,128)} %convolution_bitcast_fusion.4) | copy-start | bytes 786436
  371.4 7.7 %copy-start.78 = (f32[1,256,256]{2,1,0:T(8,128)S(1)}, f32[1,256,256]{2,1,0:T(8,128)}, u32[]{:S(2)}) copy-start(f32[1,256,256]{2,1,0:T(8,128)} %convolution_bitcast_fusion.6) | copy-start | bytes 786436
  371.4 7.7 %copy-start.79 = (f32[1,256,256]{2,1,0:T(8,128)S(1)}, f32[1,256,256]{2,1,0:T(8,128)}, u32[]{:S(2)}) copy-start(f32[1,256,256]{2,1,0:T(8,128)} %convolution_bitcast_fusion.5) | copy-start | bytes 786436
  371.4 7.7 %copy-start.82 = (f32[1,256,256]{2,1,0:T(8,128)S(1)}, f32[1,256,256]{2,1,0:T(8,128)}, u32[]{:S(2)}) copy-start(f32[1,256,256]{2,1,0:T(8,128)} %convolution_bitcast_fusion.3) | copy-start | bytes 786436
  381.5 34.3 %copy-start.23 = (f32[4,8,64,64]{2,3,1,0:T(8,128)S(1)}, f32[4,8,64,64]{2,3,1,0:T(8,128)}, u32[]{:S(2)}) copy-start(f32[4,8,64,64]{2,3,1,0:T(8,128)} %copy-done.22) | copy-start | bytes 1572868
  381.5 34.3 %copy-start.123 = (f32[4,8,64]{2,1,0:T(8,128)S(1)}, f32[4,8,64]{2,1,0:T(8,128)}, u32[]{:S(2)}) copy-start(f32[4,8,64]{2,1,0:T(8,128)} %copy-done.122) | copy-start | bytes 24580
  382.1 33.7 %copy-start.161 = (f32[4,8,64]{2,1,0:T(8,128)S(1)}, f32[4,8,64]{2,1,0:T(8,128)}, u32[]{:S(2)}) copy-start(f32[4,8,64]{2,1,0:T(8,128)} %multiply_divide_fusion.3) | copy-start | bytes 24580
  384.7 33.5 %copy-start.160 = (f32[4,8,64]{2,1,0:T(8,128)S(1)}, f32[4,8,64]{2,1,0:T(8,128)}, u32[]{:S(2)}) copy-start(f32[4,8,64]{2,1,0:T(8,128)} %copy-done.159) | copy-start | bytes 24580
  (235 other events, 526.1 us)
Sparse Core Ops, SparseCore 0:
  59.8 32.4 all-reduce.74
  172.8 33.1 all-reduce.76
  279.3 33.4 all-reduce.78
  382.3 33.4 all-reduce.80
